TPU v7x, 32 devices: a whole 2x2x4 slice. The times are simulated.
32 devices in a mesh: video: 8 (over y, x, core), head: 4 (over z).
Axes of the slice: x: 2, y: 2, z: 4, core: 2. Of those that a mesh axis runs over, the one named last changes fastest.
Arguments:
- text_queries: bfloat16 [128, 8192], P('video', 'head'), may hold values from -140 to 140
- visual_keys: bfloat16 [4096, 1024], P('video', 'head'), may hold values from -5 to 5
- visual_values: bfloat16 [4096, 1024], P('video', 'head'), may hold values from -6 to 6
- out_grad: bfloat16 [128, 8192], P('video', 'head'), may hold values from -384 to 384
- query_frame: int32 [128], replicated, may hold values from 0 to 15
- block_frame: int32 [32], replicated, may hold values from 0 to 16, as said below
- q_weight: bfloat16 [8192, 8192], P('head', 'video'), may hold values from -0.0625 to 0.0625
Outputs:
- query_grad: bfloat16 [128, 8192], P('video', 'head')
- key_grad: bfloat16 [4096, 1024], P('video', 'head')
- value_grad: bfloat16 [4096, 1024], P('video', 'head')
- text_grad: bfloat16 [128, 8192], P('head', 'video')
Inputs may be any that keep to these rules, and one draw needn't show every extreme that they name: `block_frame`: on each index of video the first 1 to 4 block slots are live and the rest empty; some index has all 4 live. Live blocks carry frame numbers that never fall along the whole array and start at 0; empty slots carry 16.
All inputs are finite; a program needn't handle non-finite values.
Results may differ from a plain program's by a relative error of at most 0.0058.
Values may be sent and summed in bfloat16 or wider, within the bound.
A program may use at most 384 MiB of HBM per device.

v0:
```python
import jax
import jax.numpy as jnp
from jax import lax
from jax.sharding import PartitionSpec as P

HEADS = 64
KV_HEADS = 8
HEAD_DIM = 128
BLOCK = 128


neg_fill = -1e30


def joined(x, axis, combine):
    everything = jax.tree.map(lambda part: lax.all_gather(part, axis), x)
    first = jax.tree.map(lambda part: part[0], everything)

    def step(k, so_far):
        return combine(so_far, jax.tree.map(lambda part: part[k], everything))

    return lax.fori_loop(1, lax.axis_size(axis), step, first)


def split_queries(source):
    return source.reshape(source.shape[0], -1, HEADS // KV_HEADS, HEAD_DIM)


def row_frames(block_frame, row_start, piece_rows):
    row_index = row_start + jnp.arange(piece_rows, dtype=jnp.int32)
    return jnp.take(block_frame, row_index // BLOCK)


def key_layout(key_piece, value_piece, frame_rows):
    piece_rows = key_piece.shape[0]
    block_rows = BLOCK
    block_count = piece_rows // block_rows
    local_heads = key_piece.shape[1] // HEAD_DIM
    shaped_keys = key_piece.reshape(block_count, block_rows, local_heads, HEAD_DIM)
    shaped_values = value_piece.reshape(block_count, block_rows, local_heads, HEAD_DIM)
    return (shaped_keys, shaped_values, frame_rows.reshape(block_count, block_rows))


def masked_scores(query_heads, query_limit, key_block, frame_block):
    scores = jnp.einsum(
        "rgjd,kgd->rgjk", query_heads, key_block, preferred_element_type=jnp.float32
    ) * HEAD_DIM ** (-0.5)
    visible = (frame_block[None, :] <= query_limit[:, None])[:, None, None, :]
    return (jnp.where(visible, scores, neg_fill), visible)


def sweep(block_step, running, layout, grads_in):
    shaped_keys, shaped_values, shaped_frames = layout

    def visit_block(state_now, block_items):
        key_block, value_block, frame_block, grads_block = block_items
        return block_step(state_now, key_block, value_block, frame_block, grads_block)

    return lax.scan(visit_block, running, (shaped_keys, shaped_values, shaped_frames, grads_in))


def forward_step(query_heads, query_limit):

    def block_step(running, key_block, value_block, frame_block, grads_in):
        peaks, totals, weighted = running
        scores, visible = masked_scores(query_heads, query_limit, key_block, frame_block)
        new_peak = jnp.maximum(peaks, jnp.max(scores, axis=-1))
        rescale = jnp.exp(peaks - new_peak)
        weights = jnp.where(visible, jnp.exp(scores - new_peak[..., None]), 0.0)
        totals = totals * rescale + jnp.sum(weights, axis=-1)
        weighted = weighted * rescale[..., None] + jnp.einsum(
            "rgjk,kgd->rgjd",
            weights,
            value_block.astype(jnp.float32),
            precision=lax.Precision.HIGHEST,
        )
        return ((new_peak, totals, weighted), grads_in)

    return block_step


def backward_step(query_heads, grad_heads, query_limit, log_total, row_dots):

    def block_step(running, key_block, value_block, frame_block, grads_in):
        scores, visible = masked_scores(query_heads, query_limit, key_block, frame_block)
        weights = jnp.where(visible, jnp.exp(scores - log_total[..., None]), 0.0)
        value_dots = jnp.einsum(
            "rgjd,kgd->rgjk", grad_heads, value_block, preferred_element_type=jnp.float32
        )
        score_grads = (weights * (value_dots - row_dots[..., None])).astype(jnp.bfloat16)
        running = running + jnp.einsum(
            "rgjk,kgd->rgjd", score_grads, key_block, preferred_element_type=jnp.float32
        ) * HEAD_DIM ** (-0.5)
        weight_half = weights.astype(jnp.bfloat16)
        key_part = jnp.einsum(
            "rgjk,rgjd->kgd", score_grads, query_heads, preferred_element_type=jnp.float32
        ) * HEAD_DIM ** (-0.5)
        value_part = jnp.einsum(
            "rgjk,rgjd->kgd", weight_half, grad_heads, preferred_element_type=jnp.float32
        )
        grads_in = (grads_in[0] + key_part, grads_in[1] + value_part)
        return (running, grads_in)

    return block_step


def initial_state(total_rows, local_heads):
    group_size = HEADS // KV_HEADS
    return (
        jnp.full((total_rows, local_heads, group_size), neg_fill, jnp.float32),
        jnp.zeros((total_rows, local_heads, group_size), jnp.float32),
        jnp.zeros((total_rows, local_heads, group_size, HEAD_DIM), jnp.float32),
    )


def combine_parts(earlier, later):
    new_peak = jnp.maximum(earlier[0], later[0])
    early_scale = jnp.exp(earlier[0] - new_peak)
    late_scale = jnp.exp(later[0] - new_peak)
    totals = earlier[1] * early_scale + later[1] * late_scale
    weighted = earlier[2] * early_scale[..., None] + later[2] * late_scale[..., None]
    return (new_peak, totals, weighted)


def shards(text_queries, visual_keys, visual_values, out_grad, query_frame, block_frame, q_weight):
    query_rows = text_queries.shape[0]
    key_rows = visual_keys.shape[0]
    local_heads = visual_keys.shape[1] // HEAD_DIM
    video_index = lax.axis_index("video")
    own_frames = row_frames(block_frame, video_index * key_rows, key_rows)
    own_layout = key_layout(visual_keys, visual_values, own_frames)
    grad_shape = own_layout[0].shape[:2] + (local_heads, HEAD_DIM)
    all_queries, all_grads = (
        lax.all_gather(text_queries, "video", axis=0, tiled=True),
        lax.all_gather(out_grad, "video", axis=0, tiled=True),
    )
    total_rows = all_queries.shape[0]
    query_heads = split_queries(all_queries)
    grad_heads = split_queries(all_grads)
    partial_value, unused = sweep(
        forward_step(query_heads, query_frame),
        initial_state(total_rows, local_heads),
        own_layout,
        (),
    )
    peaks, totals, weighted = joined(partial_value, "video", combine_parts)
    row_dots = jnp.sum(grad_heads * (weighted / totals[..., None]), axis=-1)
    log_total = peaks + jnp.log(totals)
    zero_grads = (jnp.zeros(grad_shape, jnp.float32), jnp.zeros(grad_shape, jnp.float32))
    query_start = jnp.zeros(partial_value[2].shape, jnp.float32)
    block_step = backward_step(query_heads, grad_heads, query_frame, log_total, row_dots)
    query_sum, key_value = sweep(block_step, query_start, own_layout, zero_grads)
    query_total = lax.psum(query_sum, "video")
    query_grad_all = query_total.reshape(total_rows, -1).astype(jnp.bfloat16)
    query_grad = lax.dynamic_slice_in_dim(query_grad_all, video_index * query_rows, query_rows, 0)
    key_sum, value_sum = key_value
    key_grad = key_sum.reshape(key_rows, -1).astype(jnp.bfloat16)
    value_grad = value_sum.reshape(key_rows, -1).astype(jnp.bfloat16)
    partial_text = jnp.dot(query_grad_all, q_weight, preferred_element_type=jnp.float32)
    text_grad = lax.psum_scatter(partial_text, "head", scatter_dimension=0, tiled=True).astype(
        jnp.bfloat16
    )
    return (query_grad, key_grad, value_grad, text_grad)


def solution(mesh):
    in_specs = (
        P("video", "head"),
        P("video", "head"),
        P("video", "head"),
        P("video", "head"),
        P(),
        P(),
        P("head", "video"),
    )
    out_specs = (P("video", "head"), P("video", "head"), P("video", "head"), P("head", "video"))
    return jax.shard_map(shards, mesh=mesh, in_specs=in_specs, out_specs=out_specs, check_vma=False)
```

profile of v0, /device:TPU:0, one launch (start us, length us, event | category | flops | bytes accessed | tf_op | source)
XLA Modules:
  0.0 251.3 jit_solution(603322872081449320)
XLA Ops:
  9.1 2.1 fusion.44
  11.7 11.6 %all_gather.24 = bf16[128,2048]{1,0:T(8,128)(2,1)S(1)} all-gather(bf16[16,2048]{1,0:T(8,128)(2,1)} %param.13), channel_id=1, replica_groups=mesh['video'=8,'head'=4] {'video'}, dimensions={0}, use_global_device_ids=true | all-gather | bytes 589824 | tf_op jit(solution)/shard_map/all_gather | solution.py:134
  26.0 4.3 %compare_select_fusion.1 = s32[512,1]{0,1:T(1,128)S(1)} fusion(s32[]{:T(128)} %bitcast.28, s32[]{:T(128)} %bitcast.29, s32[]{:T(128)} %bitcast.30, s32[]{:T(128)} %bitcast.31, s32[]{:T(128)} %bitcast.32, s32[]{:T(128)} %bitcast.34, s32[]{:T(128)} %bitcast.33, s32[]{:T(128)S(6)} %mul.119), kind=kLoop, calls=%fused_computation.93 | loop fusion | flops 15872 | bytes 2080 | tf_op jit(solution)/shard_map/jit(_take)/gather | solution.py:31
  30.3 15.8 %bitcast_select_fusion = s32[4,128]{1,0:T(4,128)S(1)} fusion(pred[512]{0:T(512)(128)(4,1)S(1)} %get-tuple-element.541, pred[512]{0:T(512)(128)(4,1)S(1)} %get-tuple-element.542, pred[512]{0:T(512)(128)(4,1)S(1)} %get-tuple-element.543, pred[512]{0:T(512)(128)(4,1)S(1)} %get-tuple-element.544, pred[512]{0:T(512)(128)(4,1)S(1)} %get-tuple-element.545, ...), kind=kLoop, calls=%fused_computation.109 | loop fusion | flops 25600 | bytes 17000 | tf_op jit(solution)/shard_map/jit(_take)/select_n | solution.py:31
  46.1 7.8 %while.50 = (s32[]{:T(128)}, f32[128,2,8]{0,2,1:T(8,128)S(1)}, f32[128,2,8]{0,2,1:T(8,128)S(1)}, f32[128,2,8,128]{0,3,2,1:T(8,128)S(1)}, s32[4,128]{1,0:T(4,128)...) while((s32[]{:T(128)}, f32[128,2,8]{0,2,1:T(8,128)S(1)}, ...), condition=%wide.region_3.4_spmd.clone, body=%wide.region_0.0_spmd.clone.sunk | while | flops 472672256 | bytes 6359173 | solution.py:59
  55.0 8.8 %all-gather = f32[1024,2,8]{0,2,1:T(8,128)S(1)} all-gather(f32[128,2,8]{0,2,1:T(8,128)S(1)} %get-tuple-element.295), channel_id=2, replica_groups=mesh['video'=8,'head'=4] {'video'}, dimensions={0}, use_global_device_ids=true | all-gather | bytes 73728 | tf_op jit(solution)/shard_map/all_gather | solution.py:16
  63.8 10.1 %all-gather.1 = f32[1024,2,8]{0,2,1:T(8,128)} all-gather(f32[128,2,8]{0,2,1:T(8,128)S(1)} %get-tuple-element.296), channel_id=3, replica_groups=mesh['video'=8,'head'=4] {'video'}, dimensions={0}, use_global_device_ids=true | all-gather | bytes 73728 | tf_op jit(solution)/shard_map/all_gather | solution.py:16
  74.6 9.6 %all_gather.31 = bf16[128,2048]{1,0:T(8,128)(2,1)S(1)} all-gather(bf16[16,2048]{1,0:T(8,128)(2,1)S(1)} %copy-done.5), channel_id=1, replica_groups=mesh['video'=8,'head'=4] {'video'}, dimensions={0}, use_global_device_ids=true | all-gather | bytes 589824 | tf_op jit(solution)/shard_map/all_gather | solution.py:135
  84.8 26.7 %all-gather.5.cloned.1.call-done = f32[1024,2,8,128]{0,3,2,1:T(8,128)} async-done(((f32[128,2,8,128]{0,3,2,1:T(8,128)}), f32[1024,2,8,128]{0,3,2,1:T(8,128)}) %all-gather.5.cloned.1.call-update) | async-done | bytes 8388624 | tf_op jit(solution)/shard_map/all_gather | solution.py:16
  111.4 2.4 slice.50
  115.6 9.2 %copy.78 = f32[1024,2,8,128]{3,2,1,0:T(8,128)} copy(f32[1024,2,8,128]{0,3,2,1:T(8,128)} %all-gather.5.cloned.1.call-done) | data formatting | bytes 16777216 | tf_op jit(solution)/shard_map/while | solution.py:22
  124.8 20.6 %while.49 = (s32[]{:T(128)}, f32[128,2,8]{0,2,1:T(8,128)S(1)}, f32[128,2,8]{0,2,1:T(8,128)S(1)}, f32[128,2,8,128]{3,2,1,0:T(8,128)S(1)}, f32[8,128,2,8]{1,3,0,2:...) while((s32[]{:T(128)}, f32[128,2,8]{0,2,1:T(8,128)S(1)}, ...), condition=%wide.region_5.6_spmd, body=%wide.region_4.5_spmd.sunk | while | flops 798725 | bytes 3260567 | solution.py:22
  128.7 1.9 fusion.81
  131.6 1.9 fusion.81
  134.6 1.9 fusion.81
  137.5 1.9 fusion.81
  143.4 1.9 fusion.81
  148.1 17.7 %while.51 = (s32[]{:T(128)}, f32[128,2,8,128]{0,3,2,1:T(8,128)}, bf16[4,128,2,128]{3,1,2,0:T(8,128)(2,1)}, bf16[4,128,2,128]{3,1,2,0:T(8,128)(2,1)}, bf16[4,128,...) while((s32[]{:T(128)}, f32[128,2,8,128]{0,3,2,1:T(8,128)}, ...), condition=%wide.region_8.9_spmd.clone, body=%wide.region_7.8_spmd.clone.sunk | while | flops 338477056 | bytes 11651803 | solution.py:59
  152.6 2.6 %fusion.101 = f32[128,2,8,128]{0,3,2,1:T(8,128)} fusion(bf16[128,2,8,128]{0,3,2,1:T(8,128)(2,1)S(1)} %fusion.100, f32[128,2,8,128]{0,3,2,1:T(8,128)} %get-tuple-element.830, pred[]{:T(512)S(6)} %compare.148, bf16[4,128,2,128]{3,1,2,0:T(8,128)(2,1)S(1)} %get-tuple-element.847, s32[]{:T(128)} %get-tuple-element.829), kind=kOutput, calls=%fused_computation.37.clone.1 | convolution fusion | flops 67895296 | bytes 2686981 | tf_op jit(solution)/shard_map/while/body/eval_jaxpr/rgjk,kgd->rgjd/dot_general | solution.py:91
  157.3 2.6 %fusion.101 = f32[128,2,8,128]{0,3,2,1:T(8,128)} fusion(bf16[128,2,8,128]{0,3,2,1:T(8,128)(2,1)S(1)} %fusion.100, f32[128,2,8,128]{0,3,2,1:T(8,128)} %get-tuple-element.830, pred[]{:T(512)S(6)} %compare.148, bf16[4,128,2,128]{3,1,2,0:T(8,128)(2,1)S(1)} %get-tuple-element.847, s32[]{:T(128)} %get-tuple-element.829), kind=kOutput, calls=%fused_computation.37.clone.1 | convolution fusion | flops 67895296 | bytes 2686981 | tf_op jit(solution)/shard_map/while/body/eval_jaxpr/rgjk,kgd->rgjd/dot_general | solution.py:91
  162.0 2.6 %fusion.101 = f32[128,2,8,128]{0,3,2,1:T(8,128)} fusion(bf16[128,2,8,128]{0,3,2,1:T(8,128)(2,1)S(1)} %fusion.100, f32[128,2,8,128]{0,3,2,1:T(8,128)} %get-tuple-element.830, pred[]{:T(512)S(6)} %compare.148, bf16[4,128,2,128]{3,1,2,0:T(8,128)(2,1)S(1)} %get-tuple-element.847, s32[]{:T(128)} %get-tuple-element.829), kind=kOutput, calls=%fused_computation.37.clone.1 | convolution fusion | flops 67895296 | bytes 2686981 | tf_op jit(solution)/shard_map/while/body/eval_jaxpr/rgjk,kgd->rgjd/dot_general | solution.py:91
  165.8 50.5 %all-reduce.1 = bf16[128,2,8,128]{0,3,2,1:T(8,128)(2,1)S(1)} all-reduce(f32[128,2,8,128]{0,3,2,1:T(8,128)} %get-tuple-element.301), channel_id=1, replica_groups=mesh['video'=8,'head'=4] {'video'}, use_global_device_ids=true, to_apply=%region_9.10 | all-reduce | flops 262144 | bytes 1572864 | tf_op jit(solution)/shard_map/psum | solution.py:153
  216.3 3.8 %fusion.46 = f32[128,1024]{1,0:T(8,128)} fusion(bf16[128,2048]{0,1:T(8,128)(2,1)S(1)} %bitcast.218, bf16[2048,1024]{1,0:T(8,128)(2,1)} %param.19), kind=kOutput, calls=%fused_computation.118 | convolution fusion | flops 536870912 | bytes 5242880 | tf_op jit(solution)/shard_map/dot_general | solution.py:159
  223.2 19.8 %reduce-scatter.2.cloned.1.call-done = f32[32,1024]{1,0:T(8,128)} async-done(((f32[128,1024]{1,0:T(8,128)}), f32[32,1024]{1,0:T(8,128)}) %reduce-scatter.2.cloned.1.call-update) | async-done | bytes 131088 | tf_op jit(solution)/shard_map/reduce_scatter | solution.py:160
  (162 shorter events, 44.5 us)
Async XLA Ops:
  7.2 38.9 %copy-start.6 = (s32[128]{0:T(128)S(1)}, s32[128]{0:T(128)}, u32[]{:S(2)}) copy-start(s32[128]{0:T(128)} %param.17) | copy-start | bytes 1540
  7.2 104.3 %all-gather.5.cloned.1.call-start = ((), (), s32[]{:S(2)}) async-start(), calls=%async_computation.2 | async-start | bytes 9437184 | tf_op jit(solution)/shard_map/all_gather | solution.py:16
  46.1 28.5 %copy-start.5 = (bf16[16,2048]{1,0:T(8,128)(2,1)S(1)}, bf16[16,2048]{1,0:T(8,128)(2,1)}, u32[]{:S(2)}) copy-start(bf16[16,2048]{1,0:T(8,128)(2,1)} %param.16) | copy-start | bytes 196612
  53.9 1.1 copy-start
  55.0 188.0 %reduce-scatter.2.cloned.1.call-start = ((), (), s32[]{:S(2)}) async-start(), calls=%async_computation.1 | async-start | bytes 655360 | tf_op jit(solution)/shard_map/reduce_scatter | solution.py:160
  148.1 2.3 copy-start.1
  150.7 0.9 copy-start.2
  151.7 3.5 %copy-start.1 = (bf16[4,128,2,128]{3,1,2,0:T(8,128)(2,1)S(1)}, bf16[4,128,2,128]{3,1,2,0:T(8,128)(2,1)}, u32[]{:S(2)}) copy-start(bf16[4,128,2,128]{3,1,2,0:T(8,128)(2,1)} %get-tuple-element.831) | copy-start | bytes 786436 | tf_op jit(solution)/shard_map/while
  155.4 0.9 copy-start.2
  156.4 3.5 %copy-start.1 = (bf16[4,128,2,128]{3,1,2,0:T(8,128)(2,1)S(1)}, bf16[4,128,2,128]{3,1,2,0:T(8,128)(2,1)}, u32[]{:S(2)}) copy-start(bf16[4,128,2,128]{3,1,2,0:T(8,128)(2,1)} %get-tuple-element.831) | copy-start | bytes 786436 | tf_op jit(solution)/shard_map/while
  160.2 0.9 copy-start.2
  161.1 3.5 %copy-start.1 = (bf16[4,128,2,128]{3,1,2,0:T(8,128)(2,1)S(1)}, bf16[4,128,2,128]{3,1,2,0:T(8,128)(2,1)}, u32[]{:S(2)}) copy-start(bf16[4,128,2,128]{3,1,2,0:T(8,128)(2,1)} %get-tuple-element.831) | copy-start | bytes 786436 | tf_op jit(solution)/shard_map/while
  164.9 0.9 copy-start.2
  165.8 55.3 %copy-start.4 = (bf16[4,128,2,128]{3,1,2,0:T(8,128)(2,1)S(1)}, bf16[4,128,2,128]{3,1,2,0:T(8,128)(2,1)}, u32[]{:S(2)}) copy-start(bf16[4,128,2,128]{3,1,2,0:T(8,128)(2,1)} %get-tuple-element.303) | copy-start | bytes 786436
  216.3 5.8 %copy-start.3 = (bf16[4,128,2,128]{3,1,2,0:T(8,128)(2,1)S(1)}, bf16[4,128,2,128]{3,1,2,0:T(8,128)(2,1)}, u32[]{:S(2)}) copy-start(bf16[4,128,2,128]{3,1,2,0:T(8,128)(2,1)} %get-tuple-element.302) | copy-start | bytes 786436
Sparse Core Ops, SparseCore 0:
  55.1 56.2 all-gather.4
  220.2 22.6 reduce-scatter.1
where the time goes:
time: 253 us; the launch traced here: 251 us
  blocking collectives  90.5 us (36%)
  waiting for transfers between devices  46.5 us (18%)
  other arithmetic  43.3 us (17%)
  local copies, waits for them, and re-layouts  29.7 us (12%)
  matrix products  26.1 us (10%)
  between operations  14.3 us (6%)
    psum x1, blocking collectives, shards(): query_total = lax.psum(query_sum, 'video')  50.5 us
    all_gather x1, waiting for transfers between devices, joined(): everything = jax.tree.map(lambda part: lax.all_gather(part, axis), x)  26.7 us
    reduce_scatter x1, waiting for transfers between devices, shards(): lax.psum_scatter(partial_text, 'head', scatter_dimension=0, tiled=True)  19.8 us
    all_gather x2, blocking collectives, joined(): everything = jax.tree.map(lambda part: lax.all_gather(part, axis), x)  18.9 us
    select_n x1, other arithmetic, row_frames(): return jnp.take(block_frame, row_index // BLOCK)  15.8 us
    add x7, other arithmetic, combine_parts(): earlier[2] * early_scale[..., None] + later[2] * late_scale[..., None]  13.3 us
    while x3, local copies, waits for them, and re-layouts, joined(): return lax.fori_loop(1, lax.axis_size(axis), step, first)  12.3 us
    all_gather x1, blocking collectives, shards(): lax.all_gather(text_queries, 'video', axis=0, tiled=True)  11.6 us
  transfers between devices with their start and end apart: 2, of which 2 were waited for; matrix products, arithmetic and copies ran while one was open for 2% of the time, Pallas kernels for 0%

commit v1 on v0

v1 whole, which is shorter than its diff:
```python
import functools

import jax
import jax.numpy as jnp
from jax import lax
from jax.experimental import pallas as pl
from jax.experimental.pallas import tpu as pltpu
from jax.sharding import PartitionSpec as P

HEADS = 64
KV_HEADS = 8
HEAD_DIM = 128
BLOCK = 128
GROUP = HEADS // KV_HEADS
CH = 4
FAR = -1.0e30
SCALE = HEAD_DIM ** (-0.5)
NT = (((1,), (1,)), ((), ()))
F32 = jnp.float32
BF16 = jnp.bfloat16


def kernel(
    V, H, qf_ref, bf_ref, q_ref, do_ref, k_ref, v_ref, w_ref,
    qg_out, kg_out, vg_out, tg_out,
    land, keys, vals, keysT, wts, bias, probs, dots, peaks, stats, coef, dqp, dqs, own, rsb, rsl,
    qg, acc, tb, tl, tout, kacc, vacc, kout, vout,
    load_sem, own_sem, out_sem, qout_sem,
    g_send, g_recv, f_send, f_recv, st_send, st_recv, x_send, x_recv, r_send, r_recv,
    a_send, a_recv, b_send, b_recv, z_send, z_recv,
):
    C = V // 2
    me = lax.axis_index("video")
    z = lax.axis_index("head")
    c = me // 2
    core = lax.rem(me, 2)
    mate = c * 2 + (1 - core)
    K = land.shape[0]
    R = q_ref.shape[0]
    NQ = V * R
    T = k_ref.shape[0]
    NB = T // BLOCK
    G = k_ref.shape[1] // HEAD_DIM
    CW = CH * HEAD_DIM
    NW = w_ref.shape[1]
    CZ = C // H
    ins = (q_ref, do_ref)

    def local(src, dst, sem):
        return pltpu.make_async_copy(src, dst, sem)

    def remote(src, dst, ssem, rsem, axis, target):
        pltpu.make_async_remote_copy(
            src_ref=src, dst_ref=dst, send_sem=ssem, recv_sem=rsem,
            device_id={axis: target}, device_id_type=pl.DeviceIdType.MESH,
        ).start()

    def wait(ref, sem):
        pltpu.make_async_copy(ref, ref, sem).wait()

    for k in range(K):
        for a in range(2):
            local(ins[a].at[:, pl.ds(k * CW, CW)], land.at[k, a, core, c], own_sem.at[k, a]).start()
    local(k_ref, keys, load_sem.at[0]).start()
    local(v_ref, vals, load_sem.at[1]).start()
    local(w_ref, wts, load_sem.at[2]).start()

    barrier = pltpu.get_barrier_semaphore()
    for o in range(1, V):
        pl.semaphore_signal(
            barrier, inc=1, device_id={"video": lax.rem(me + o, V)},
            device_id_type=pl.DeviceIdType.MESH,
        )
    for o in range(1, H):
        pl.semaphore_signal(
            barrier, inc=1, device_id={"head": lax.rem(z + o, H)},
            device_id_type=pl.DeviceIdType.MESH,
        )
    pl.semaphore_wait(barrier, V - 1 + H - 1)

    chips = [lax.rem(c + o, C) for o in range(1, C)]

    for k in range(K):
        for a in range(2):
            for cc in chips:
                remote(
                    ins[a].at[:, pl.ds(k * CW, CW)], land.at[k, a, core, c],
                    g_send.at[k, a], g_recv.at[k, a], "video", cc * 2 + core,
                )

    for b in range(NB):
        seen = bf_ref[me * NB + b] <= qf_ref[...]
        bias[pl.ds(b, 1), :] = jnp.where(seen, 0.0, FAR).astype(F32)
    wait(keys, load_sem.at[0])
    for g in range(G):
        part = keys[:, g * HEAD_DIM:(g + 1) * HEAD_DIM].astype(F32)
        keysT[g] = part.T.astype(BF16)
    wait(vals, load_sem.at[1])

    def arrive(k):
        for a in range(2):
            wait(land.at[k, a, core, c], own_sem.at[k, a])
            wait(land.at[k, a, core, pl.ds(0, C - 1)], g_recv.at[k, a])
            remote(
                land.at[k, a, core], land.at[k, a, core],
                f_send.at[k, a], f_recv.at[k, a], "video", mate,
            )

    def heads_of(k, a, hh):
        cols = pl.ds(pl.multiple_of(hh * HEAD_DIM, HEAD_DIM), HEAD_DIM)
        return land[k, a, :, :, :, cols].reshape(NQ, HEAD_DIM)

    def group_of(k):
        return (k * CH) // GROUP

    def forward(k):
        for a in range(2):
            wait(land.at[k, a, 1 - core], f_recv.at[k, a])
        g = group_of(k)
        feats = slice(g * HEAD_DIM, (g + 1) * HEAD_DIM)

        def head(hh, carry):
            s = lax.dot_general(keys[:, feats], heads_of(k, 0, hh), NT, preferred_element_type=F32)
            s = s.reshape(NB, BLOCK, NQ) * SCALE + bias[...].reshape(NB, 1, NQ)
            s = s.reshape(T, NQ)
            m = jnp.max(s, axis=0, keepdims=True)
            m = jnp.where(m > 0.1 * FAR, m, 0.0)
            p = jnp.exp(s - m)
            total = jnp.sum(p, axis=0, keepdims=True)
            d = lax.dot_general(vals[:, feats], heads_of(k, 1, hh), NT, preferred_element_type=F32)
            r = jnp.sum(p * d, axis=0, keepdims=True)
            probs[k * CH + hh] = p
            dots[k * CH + hh] = d
            live = total > 0.0
            safe = jnp.where(live, total, 1.0)
            peaks[k, pl.ds(hh, 1), :] = m
            stats[k, me, pl.ds(hh, 1), :] = jnp.where(live, m + jnp.log(safe), FAR)
            stats[k, me, pl.ds(CH + hh, 1), :] = r / safe
            return carry

        lax.fori_loop(0, CH, head, 0)
        for o in range(1, V):
            remote(
                stats.at[k, me], stats.at[k, me], st_send.at[k], st_recv.at[k],
                "video", lax.rem(me + o, V),
            )

    def weights_of(k, hh):
        w = probs[k * CH + hh] * coef[k, pl.ds(hh, 1), :]
        ds = w * (dots[k * CH + hh] - coef[k, pl.ds(CH + hh, 1), :])
        return w, ds.astype(BF16)

    def backward(k):
        wait(stats.at[k, pl.ds(0, V - 1)], st_recv.at[k])
        parts = stats[k]
        logs, rows = parts[:, :CH], parts[:, CH:]
        top = jnp.max(logs, axis=0)
        e = jnp.exp(logs - top[None])
        total = jnp.sum(e, axis=0)
        log_total = top + jnp.log(total)
        coef[k, pl.ds(0, CH), :] = jnp.exp(jnp.minimum(peaks[k] - log_total, 0.0))
        coef[k, pl.ds(CH, CH), :] = jnp.sum(e * rows, axis=0) / total
        g = group_of(k)

        def head(hh, carry):
            w, ds = weights_of(k, hh)
            dqT = jnp.dot(keysT[g], ds, preferred_element_type=F32)
            cols = pl.ds(pl.multiple_of(hh * HEAD_DIM, HEAD_DIM), HEAD_DIM)
            dqp[k, :, :, :, cols] = dqT.T.reshape(2, C, R, HEAD_DIM)
            return carry

        lax.fori_loop(0, CH, head, 0)
        remote(dqp.at[k, 1 - core], dqs.at[k], x_send.at[k], x_recv.at[k], "video", mate)

    def pair_sum(k):
        wait(dqs.at[k], x_recv.at[k])
        s = dqp[k, core] + dqs[k]
        own[k] = s
        rsb[k] = s.astype(BF16)
        for cc in chips:
            remote(
                rsb.at[k, cc], rsl.at[k, c], r_send.at[k], r_recv.at[k], "video", cc * 2 + core
            )

    def total_sum(k):
        wait(rsl.at[k, pl.ds(0, C - 1)], r_recv.at[k])
        s = own[k, c]
        for cc in chips:
            s = s + rsl[k, cc].astype(F32)
        qg[k, core, c] = (s * SCALE).astype(BF16)
        for cc in chips:
            remote(
                qg.at[k, core, c], qg.at[k, core, c], a_send.at[k], a_recv.at[k],
                "video", cc * 2 + core,
            )
        local(qg.at[k, core, c], qg_out.at[:, pl.ds(k * CW, CW)], qout_sem.at[k]).start()

    def spread(k):
        wait(qg.at[k, core, pl.ds(0, C - 1)], a_recv.at[k])
        remote(qg.at[k, core], qg.at[k, core], b_send.at[k], b_recv.at[k], "video", mate)

    def text(k):
        wait(qg.at[k, 1 - core], b_recv.at[k])
        if k == 0:
            wait(wts, load_sem.at[2])
        x = qg[k].reshape(NQ, CW)
        part = jnp.dot(x, wts[k * CW:(k + 1) * CW, :], preferred_element_type=F32)
        part = part.reshape(2, C, R, NW)
        if k > 0:
            part = part + acc[...]
        if k < K - 1:
            acc[...] = part
        else:
            acc[...] = part
            tb[...] = part.astype(BF16)

    def key_value(k):
        g = group_of(k)
        fresh = (k * CH) % GROUP == 0
        last = ((k + 1) * CH) % GROUP == 0
        if fresh:
            kacc[...] = jnp.zeros_like(kacc)
            vacc[...] = jnp.zeros_like(vacc)

        def head(hh, carry):
            w, ds = weights_of(k, hh)
            kacc[...] += jnp.dot(ds, heads_of(k, 0, hh), preferred_element_type=F32)
            vacc[...] += jnp.dot(w.astype(BF16), heads_of(k, 1, hh), preferred_element_type=F32)
            return carry

        lax.fori_loop(0, CH, head, 0)
        if last:
            feats = pl.ds(g * HEAD_DIM, HEAD_DIM)
            kout[g] = (kacc[...] * SCALE).astype(BF16)
            vout[g] = vacc[...].astype(BF16)
            local(kout.at[g], kg_out.at[:, feats], out_sem.at[0, g]).start()
            local(vout.at[g], vg_out.at[:, feats], out_sem.at[1, g]).start()

    for k in range(K):
        arrive(k)
        if k:
            forward(k - 1)
    forward(K - 1)
    for k in range(K):
        backward(k)
        if k:
            pair_sum(k - 1)
    pair_sum(K - 1)
    for k in range(K):
        total_sum(k)
        if k < K - 2:
            key_value(k)
    for k in range(K):
        spread(k)
        if k:
            text(k - 1)
    text(K - 1)
    for o in range(1, H):
        zz = lax.rem(z + o, H)
        remote(tb.at[:, pl.ds(zz * CZ, CZ)], tl.at[z], z_send, z_recv, "head", zz)
    for k in range(max(K - 2, 0), K):
        key_value(k)
    wait(tl.at[pl.ds(0, H - 1)], z_recv)
    for i in range(CZ):
        for half in range(2):
            s = acc[half, z * CZ + i]
            for o in range(1, H):
                s = s + tl[lax.rem(z + o, H), half, i].astype(F32)
            tout[pl.ds((i * 2 + half) * R, R), :] = s.astype(BF16)
    local(tout, tg_out, load_sem.at[0]).start()

    for k in range(K):
        for a in range(2):
            wait(land.at[k, a, core, pl.ds(0, C - 1)], g_send.at[k, a])
            wait(land.at[k, a, core], f_send.at[k, a])
        wait(stats.at[k, pl.ds(0, V - 1)], st_send.at[k])
        wait(dqs.at[k], x_send.at[k])
        wait(rsl.at[k, pl.ds(0, C - 1)], r_send.at[k])
        wait(qg.at[k, core, pl.ds(0, C - 1)], a_send.at[k])
        wait(qg.at[k, core], b_send.at[k])
        wait(qg.at[k, core, c], qout_sem.at[k])
    wait(tl.at[pl.ds(0, H - 1)], z_send)
    for g in range(G):
        wait(kout.at[g], out_sem.at[0, g])
        wait(vout.at[g], out_sem.at[1, g])
    wait(tout, load_sem.at[0])


def shards(V, H, text_queries, visual_keys, visual_values, out_grad, query_frame, block_frame, q_weight):
    R, QW = text_queries.shape
    T, KW = visual_keys.shape
    C = V // 2
    NQ = V * R
    NW = q_weight.shape[1]
    HL = QW // HEAD_DIM
    G = KW // HEAD_DIM
    K = HL // CH
    CW = CH * HEAD_DIM
    CZ = C // H
    frames = query_frame.reshape(C, 2, R).transpose(1, 0, 2).reshape(1, NQ)
    vmem = pltpu.VMEM
    dma = pltpu.SemaphoreType.DMA
    any_spec = pl.BlockSpec(memory_space=pl.ANY)
    return pl.pallas_call(
        functools.partial(kernel, V, H),
        out_shape=(
            jax.ShapeDtypeStruct((R, QW), BF16),
            jax.ShapeDtypeStruct((T, KW), BF16),
            jax.ShapeDtypeStruct((T, KW), BF16),
            jax.ShapeDtypeStruct((NQ // H, NW), BF16),
        ),
        in_specs=[
            pl.BlockSpec(memory_space=pltpu.VMEM),
            pl.BlockSpec(memory_space=pltpu.SMEM),
        ] + [any_spec] * 5,
        out_specs=(any_spec,) * 4,
        scratch_shapes=[
            vmem((K, 2, 2, C, R, CW), BF16),
            vmem((T, KW), BF16),
            vmem((T, KW), BF16),
            vmem((G, HEAD_DIM, T), BF16),
            vmem((QW, NW), BF16),
            vmem((T // BLOCK, NQ), F32),
            vmem((HL, T, NQ), F32),
            vmem((HL, T, NQ), F32),
            vmem((K, CH, NQ), F32),
            vmem((K, V, 2 * CH, NQ), F32),
            vmem((K, 2 * CH, NQ), F32),
            vmem((K, 2, C, R, CW), F32),
            vmem((K, C, R, CW), F32),
            vmem((K, C, R, CW), F32),
            vmem((K, C, R, CW), BF16),
            vmem((K, C, R, CW), BF16),
            vmem((K, 2, C, R, CW), BF16),
            vmem((2, C, R, NW), F32),
            vmem((2, C, R, NW), BF16),
            vmem((H, 2, CZ, R, NW), BF16),
            vmem((NQ // H, NW), BF16),
            vmem((T, HEAD_DIM), F32),
            vmem((T, HEAD_DIM), F32),
            vmem((G, T, HEAD_DIM), BF16),
            vmem((G, T, HEAD_DIM), BF16),
            dma((3,)), dma((K, 2)), dma((2, G)), dma((K,)),
            dma((K, 2)), dma((K, 2)), dma((K, 2)), dma((K, 2)),
            dma((K,)), dma((K,)), dma((K,)), dma((K,)), dma((K,)), dma((K,)),
            dma((K,)), dma((K,)), dma((K,)), dma((K,)), dma, dma,
        ],
        compiler_params=pltpu.CompilerParams(
            collective_id=0, has_side_effects=True, vmem_limit_bytes=66_000_000
        ),
    )(frames, block_frame, text_queries, out_grad, visual_keys, visual_values, q_weight)


def solution(mesh):
    in_specs = (
        P("video", "head"),
        P("video", "head"),
        P("video", "head"),
        P("video", "head"),
        P(),
        P(),
        P("head", "video"),
    )
    out_specs = (P("video", "head"), P("video", "head"), P("video", "head"), P("head", "video"))
    body = functools.partial(shards, mesh.shape["video"], mesh.shape["head"])
    return jax.shard_map(body, mesh=mesh, in_specs=in_specs, out_specs=out_specs, check_vma=False)
```

time: 253 us -> 47.3 us (0.19)
  blocking collectives: 90.5 us -> 0 us
  waiting for transfers between devices: 46.5 us -> 0 us
  other arithmetic: 43.3 us -> 0 us
  Pallas kernels: 0 us -> 38.6 us
  matrix products: 26.1 us -> 0 us
  local copies, waits for them, and re-layouts: 29.7 us -> 7.63 us
  between operations: 14.3 us -> 0.64 us
    psum x1 -> x0, blocking collectives: 50.5 us -> none  [shards(): query_total = lax.psum(query_sum, 'video')]
    all_gather x4 -> x0, blocking collectives: 40.1 us -> none  [the longest x2 18.9 us: joined(): everything = jax.tree.map(lambda part: lax.all_gather(part, axis), x)]
    pallas_call x0 -> x1, Pallas kernels: none -> 38.6 us  [shards(): pl.pallas_call(functools.partial(kernel, V, H), out_shape=(jax.ShapeDtype...]
    all_gather x1 -> x0, waiting for transfers between devices: 26.7 us -> none  [joined(): everything = jax.tree.map(lambda part: lax.all_gather(part, axis), x)]
    dot_general x29 -> x0, matrix products: 26.1 us -> none  [the longest x4 9.08 us: block_step(): jnp.einsum('rgjk,kgd->rgjd', score_grads, key_block, preferred_element_ty...]
    reduce_scatter x1 -> x0, waiting for transfers between devices: 19.8 us -> none  [shards(): lax.psum_scatter(partial_text, 'head', scatter_dimension=0, tiled=True)]
    add x19 -> x0, other arithmetic: 18.3 us -> none  [the longest x7 13.3 us: combine_parts(): earlier[2] * early_scale[..., None] + later[2] * late_scale[..., None]]
    select_n x1 -> x0, other arithmetic: 15.8 us -> none  [row_frames(): return jnp.take(block_frame, row_index // BLOCK)]
  transfers between devices with their start and end apart: 2 -> 0, of which waited for: 2 -> 0; matrix products, arithmetic and copies ran while one was open for 2% -> 0% of each run, Pallas kernels for 0% -> 0%
where the time goes in v1:
time: 47.3 us; the launch traced here: 46.9 us
  Pallas kernels  38.6 us (82%)
  local copies, waits for them, and re-layouts  7.63 us (16%)
  between operations  0.64 us (1%)
    pallas_call x1, Pallas kernels, shards(): pl.pallas_call(functools.partial(kernel, V, H), out_shape=(jax.ShapeDtype...  38.6 us
    unnamed x4, local copies, waits for them, and re-layouts  6.28 us
    reshape x2, local copies, waits for them, and re-layouts, shards(): frames = query_frame.reshape(C, 2, R).transpose(1, 0, 2).reshape(1, NQ)  1.34 us

profile of v1, /device:TPU:0, one launch (start us, length us, event | category | flops | bytes accessed | tf_op | source)
XLA Modules:
  0.0 46.9 jit_solution(8080418797848401945)
XLA Ops:
  0.6 0.7 %reshape.14 = s32[4,2,16]{2,1,0:T(2,128)S(1)} reshape(s32[128]{0:T(128)} %param.11) | data formatting | bytes 1024 | tf_op jit(solution)/shard_map/reshape | solution.py:300
  1.4 0.6 %reshape.15.qf_ref = s32[1,128]{1,0:T(1,128)} reshape(s32[2,4,16]{2,1,0:T(4,128)S(1)} %copy.11) | data formatting | bytes 1024 | tf_op jit(solution)/shard_map/reshape | solution.py:300
  2.0 38.6 %shard_map.102 = (bf16[16,2048]{1,0:T(8,128)(2,1)}, bf16[512,256]{1,0:T(8,128)(2,1)}, bf16[512,256]{1,0:T(8,128)(2,1)}, bf16[32,1024]{1,0:T(8,128)(2,1)}) custom-call(s32[1,128]{1,0:T(1,128)} %reshape.15.qf_ref, s32[32]{0:T(128)} %bf_ref.1, bf16[16,2048]{1,0:T(8,128)(2,1)} %q_ref.1, bf16[16,2048]{1,0:T(8,128)(2,1)} %do_ref.1, bf16[512,256]{1,0:T(8,128)(2,1)} %k_ref.1, ...), custom_call_target="tpu_custom_call" | custom-call | tf_op jit(solution)/shard_map/pallas_call | solution.py:304
  40.6 1.5 %copy.16 = bf16[16,2048]{1,0:T(8,128)(2,1)} copy(bf16[16,2048]{1,0:T(8,128)(2,1)} %get-tuple-element.8) | data formatting | bytes 131072
  42.1 1.7 %copy.17 = bf16[512,256]{1,0:T(8,128)(2,1)} copy(bf16[512,256]{1,0:T(8,128)(2,1)} %get-tuple-element.9) | data formatting | bytes 524288
  43.8 1.7 %copy.18 = bf16[512,256]{1,0:T(8,128)(2,1)} copy(bf16[512,256]{1,0:T(8,128)(2,1)} %get-tuple-element.10) | data formatting | bytes 524288
  45.4 1.5 %copy.19 = bf16[32,1024]{1,0:T(8,128)(2,1)} copy(bf16[32,1024]{1,0:T(8,128)(2,1)} %get-tuple-element.11) | data formatting | bytes 131072
  (1 shorter events, 0.0 us)

commit v2 on v1

--- a/solution.py
+++ b/solution.py
@@ -13,6 +13,7 @@
 BLOCK = 128
 GROUP = HEADS // KV_HEADS
 CH = 4
+LAGS = (1, 4, 5, 8, 11, 12)
 FAR = -1.0e30
 SCALE = HEAD_DIM ** (-0.5)
 NT = (((1,), (1,)), ((), ()))
@@ -24,8 +25,8 @@
     V, H, qf_ref, bf_ref, q_ref, do_ref, k_ref, v_ref, w_ref,
     qg_out, kg_out, vg_out, tg_out,
     land, keys, vals, keysT, wts, bias, probs, dots, peaks, stats, coef, dqp, dqs, own, rsb, rsl,
-    qg, acc, tb, tl, tout, kacc, vacc, kout, vout,
-    load_sem, own_sem, out_sem, qout_sem,
+    qg, acc, tb, tl, kacc, vacc,
+    load_sem, own_sem,
     g_send, g_recv, f_send, f_recv, st_send, st_recv, x_send, x_recv, r_send, r_recv,
     a_send, a_recv, b_send, b_recv, z_send, z_recv,
 ):
@@ -82,14 +83,17 @@
 
     for k in range(K):
         for a in range(2):
+            wait(land.at[k, a, core, c], own_sem.at[k, a])
             for cc in chips:
                 remote(
-                    ins[a].at[:, pl.ds(k * CW, CW)], land.at[k, a, core, c],
+                    land.at[k, a, core, c], land.at[k, a, core, c],
                     g_send.at[k, a], g_recv.at[k, a], "video", cc * 2 + core,
                 )
 
+    rows = [qf_ref[:, (i * 2 + half) * R:(i * 2 + half + 1) * R] for half in range(2) for i in range(C)]
+    limits = jnp.concatenate(rows, axis=1)
     for b in range(NB):
-        seen = bf_ref[me * NB + b] <= qf_ref[...]
+        seen = bf_ref[me * NB + b] <= limits
         bias[pl.ds(b, 1), :] = jnp.where(seen, 0.0, FAR).astype(F32)
     wait(keys, load_sem.at[0])
     for g in range(G):
@@ -99,7 +103,6 @@
 
     def arrive(k):
         for a in range(2):
-            wait(land.at[k, a, core, c], own_sem.at[k, a])
             wait(land.at[k, a, core, pl.ds(0, C - 1)], g_recv.at[k, a])
             remote(
                 land.at[k, a, core], land.at[k, a, core],
@@ -138,7 +141,7 @@
             stats[k, me, pl.ds(CH + hh, 1), :] = r / safe
             return carry
 
-        lax.fori_loop(0, CH, head, 0)
+        lax.fori_loop(0, CH, head, 0, unroll=True)
         for o in range(1, V):
             remote(
                 stats.at[k, me], stats.at[k, me], st_send.at[k], st_recv.at[k],
@@ -169,7 +172,7 @@
             dqp[k, :, :, :, cols] = dqT.T.reshape(2, C, R, HEAD_DIM)
             return carry
 
-        lax.fori_loop(0, CH, head, 0)
+        lax.fori_loop(0, CH, head, 0, unroll=True)
         remote(dqp.at[k, 1 - core], dqs.at[k], x_send.at[k], x_recv.at[k], "video", mate)
 
     def pair_sum(k):
@@ -187,32 +190,44 @@
         s = own[k, c]
         for cc in chips:
             s = s + rsl[k, cc].astype(F32)
-        qg[k, core, c] = (s * SCALE).astype(BF16)
+        s = (s * SCALE).astype(BF16)
+        qg[k, core, c] = s
+        qg_out[:, k * CW:(k + 1) * CW] = s
         for cc in chips:
             remote(
                 qg.at[k, core, c], qg.at[k, core, c], a_send.at[k], a_recv.at[k],
                 "video", cc * 2 + core,
             )
-        local(qg.at[k, core, c], qg_out.at[:, pl.ds(k * CW, CW)], qout_sem.at[k]).start()
 
     def spread(k):
         wait(qg.at[k, core, pl.ds(0, C - 1)], a_recv.at[k])
         remote(qg.at[k, core], qg.at[k, core], b_send.at[k], b_recv.at[k], "video", mate)
 
-    def text(k):
-        wait(qg.at[k, 1 - core], b_recv.at[k])
+    def product(k, half, phase):
+        x = qg[k, half].reshape(C * R, CW)
+        part = jnp.dot(x, wts[k * CW:(k + 1) * CW, :], preferred_element_type=F32)
+        part = part.reshape(C, R, NW)
+        if k > 0:
+            part = part + acc[half]
+        acc[half] = part
+        if k == K - 1:
+            tb[half] = part.astype(BF16)
+            for o in range(1, H):
+                zz = lax.rem(z + o, H)
+                remote(
+                    tb.at[half, pl.ds(zz * CZ, CZ)], tl.at[half, z],
+                    z_send.at[phase], z_recv.at[phase], "head", zz,
+                )
+
+    def near(k):
+        spread(k)
         if k == 0:
             wait(wts, load_sem.at[2])
-        x = qg[k].reshape(NQ, CW)
-        part = jnp.dot(x, wts[k * CW:(k + 1) * CW, :], preferred_element_type=F32)
-        part = part.reshape(2, C, R, NW)
-        if k > 0:
-            part = part + acc[...]
-        if k < K - 1:
-            acc[...] = part
-        else:
-            acc[...] = part
-            tb[...] = part.astype(BF16)
+        product(k, core, 0)
+
+    def far(k):
+        wait(qg.at[k, 1 - core], b_recv.at[k])
+        product(k, 1 - core, 1)
 
     def key_value(k):
         g = group_of(k)
@@ -228,46 +243,39 @@
             vacc[...] += jnp.dot(w.astype(BF16), heads_of(k, 1, hh), preferred_element_type=F32)
             return carry
 
-        lax.fori_loop(0, CH, head, 0)
+        lax.fori_loop(0, CH, head, 0, unroll=True)
         if last:
-            feats = pl.ds(g * HEAD_DIM, HEAD_DIM)
-            kout[g] = (kacc[...] * SCALE).astype(BF16)
-            vout[g] = vacc[...].astype(BF16)
-            local(kout.at[g], kg_out.at[:, feats], out_sem.at[0, g]).start()
-            local(vout.at[g], vg_out.at[:, feats], out_sem.at[1, g]).start()
-
-    for k in range(K):
-        arrive(k)
-        if k:
-            forward(k - 1)
-    forward(K - 1)
-    for k in range(K):
-        backward(k)
-        if k:
-            pair_sum(k - 1)
-    pair_sum(K - 1)
-    for k in range(K):
-        total_sum(k)
-        if k < K - 2:
+            feats = slice(g * HEAD_DIM, (g + 1) * HEAD_DIM)
+            kg_out[:, feats] = (kacc[...] * SCALE).astype(BF16)
+            vg_out[:, feats] = vacc[...].astype(BF16)
+
+    filled = 0
+
+    def fill(upto):
+        nonlocal filled
+        for k in range(filled, min(upto, K)):
             key_value(k)
-    for k in range(K):
-        spread(k)
-        if k:
-            text(k - 1)
-    text(K - 1)
-    for o in range(1, H):
-        zz = lax.rem(z + o, H)
-        remote(tb.at[:, pl.ds(zz * CZ, CZ)], tl.at[z], z_send, z_recv, "head", zz)
-    for k in range(max(K - 2, 0), K):
-        key_value(k)
-    wait(tl.at[pl.ds(0, H - 1)], z_recv)
+        filled = max(filled, min(upto, K))
+
+    stages = (arrive, forward, backward, pair_sum, total_sum, near, far)
+    for t in range(K + LAGS[-1]):
+        for stage, lag in zip(stages, (0,) + LAGS):
+            k = t - lag
+            if 0 <= k < K:
+                stage(k)
+                if k == K - 1 and stage is pair_sum:
+                    fill(K // 2)
+                if k == K - 1 and stage is total_sum:
+                    fill(3 * K // 4)
+    fill(K)
+    wait(tl.at[core, pl.ds(0, H - 1)], z_recv.at[0])
+    wait(tl.at[1 - core, pl.ds(0, H - 1)], z_recv.at[1])
     for i in range(CZ):
         for half in range(2):
             s = acc[half, z * CZ + i]
             for o in range(1, H):
-                s = s + tl[lax.rem(z + o, H), half, i].astype(F32)
-            tout[pl.ds((i * 2 + half) * R, R), :] = s.astype(BF16)
-    local(tout, tg_out, load_sem.at[0]).start()
+                s = s + tl[half, lax.rem(z + o, H), i].astype(F32)
+            tg_out[(i * 2 + half) * R:(i * 2 + half + 1) * R, :] = s.astype(BF16)
 
     for k in range(K):
         for a in range(2):
@@ -278,12 +286,20 @@
         wait(rsl.at[k, pl.ds(0, C - 1)], r_send.at[k])
         wait(qg.at[k, core, pl.ds(0, C - 1)], a_send.at[k])
         wait(qg.at[k, core], b_send.at[k])
-        wait(qg.at[k, core, c], qout_sem.at[k])
-    wait(tl.at[pl.ds(0, H - 1)], z_send)
-    for g in range(G):
-        wait(kout.at[g], out_sem.at[0, g])
-        wait(vout.at[g], out_sem.at[1, g])
-    wait(tout, load_sem.at[0])
+    for half in range(2):
+        wait(tl.at[half, pl.ds(0, H - 1)], z_send.at[half])
+
+
+def write(*refs):
+    count = len(refs) // 2
+    sems = refs[-1]
+    copies = [
+        pltpu.make_async_copy(refs[i], refs[count + i], sems.at[i]) for i in range(count)
+    ]
+    for copy in copies:
+        copy.start()
+    for copy in copies:
+        copy.wait()
 
 
 def shards(V, H, text_queries, visual_keys, visual_values, out_grad, query_frame, block_frame, q_weight):
@@ -297,23 +313,19 @@
     K = HL // CH
     CW = CH * HEAD_DIM
     CZ = C // H
-    frames = query_frame.reshape(C, 2, R).transpose(1, 0, 2).reshape(1, NQ)
+    frames = query_frame.reshape(1, NQ)
     vmem = pltpu.VMEM
     dma = pltpu.SemaphoreType.DMA
     any_spec = pl.BlockSpec(memory_space=pl.ANY)
-    return pl.pallas_call(
+    shapes = ((R, QW), (T, KW), (T, KW), (NQ // H, NW))
+    grads = pl.pallas_call(
         functools.partial(kernel, V, H),
-        out_shape=(
-            jax.ShapeDtypeStruct((R, QW), BF16),
-            jax.ShapeDtypeStruct((T, KW), BF16),
-            jax.ShapeDtypeStruct((T, KW), BF16),
-            jax.ShapeDtypeStruct((NQ // H, NW), BF16),
-        ),
+        out_shape=tuple(vmem(shape, BF16) for shape in shapes),
         in_specs=[
             pl.BlockSpec(memory_space=pltpu.VMEM),
             pl.BlockSpec(memory_space=pltpu.SMEM),
         ] + [any_spec] * 5,
-        out_specs=(any_spec,) * 4,
+        out_specs=(pl.BlockSpec(memory_space=vmem),) * 4,
         scratch_shapes=[
             vmem((K, 2, 2, C, R, CW), BF16),
             vmem((T, KW), BF16),
@@ -334,21 +346,25 @@
             vmem((K, 2, C, R, CW), BF16),
             vmem((2, C, R, NW), F32),
             vmem((2, C, R, NW), BF16),
-            vmem((H, 2, CZ, R, NW), BF16),
-            vmem((NQ // H, NW), BF16),
+            vmem((2, H, CZ, R, NW), BF16),
             vmem((T, HEAD_DIM), F32),
             vmem((T, HEAD_DIM), F32),
-            vmem((G, T, HEAD_DIM), BF16),
-            vmem((G, T, HEAD_DIM), BF16),
-            dma((3,)), dma((K, 2)), dma((2, G)), dma((K,)),
+            dma((3,)), dma((K, 2)),
             dma((K, 2)), dma((K, 2)), dma((K, 2)), dma((K, 2)),
             dma((K,)), dma((K,)), dma((K,)), dma((K,)), dma((K,)), dma((K,)),
-            dma((K,)), dma((K,)), dma((K,)), dma((K,)), dma, dma,
+            dma((K,)), dma((K,)), dma((K,)), dma((K,)), dma((2,)), dma((2,)),
         ],
         compiler_params=pltpu.CompilerParams(
-            collective_id=0, has_side_effects=True, vmem_limit_bytes=66_000_000
+            collective_id=0, has_side_effects=True, vmem_limit_bytes=62_000_000
         ),
     )(frames, block_frame, text_queries, out_grad, visual_keys, visual_values, q_weight)
+    return pl.pallas_call(
+        write,
+        out_shape=tuple(jax.ShapeDtypeStruct(shape, BF16) for shape in shapes),
+        in_specs=[pl.BlockSpec(memory_space=vmem)] * 4,
+        out_specs=(any_spec,) * 4,
+        scratch_shapes=[dma((4,))],
+    )(*[pltpu.with_memory_space_constraint(grad, vmem) for grad in grads])
 
 
 def solution(mesh):

time: 47.3 us -> 37.2 us (0.79)
  local copies, waits for them, and re-layouts: 7.63 us -> 0 us
  Pallas kernels: 38.6 us -> 36.4 us
    unnamed x4 -> x0, local copies, waits for them, and re-layouts: 6.28 us -> none
    pallas_call x1 -> x2, Pallas kernels: 38.6 us -> 36.4 us  [the longest x1 35.5 us: shards(): pl.pallas_call(functools.partial(kernel, V, H), out_shape=tuple((vmem(sha...]
    reshape x2 -> x0, local copies, waits for them, and re-layouts: 1.34 us -> none  [shards(): frames = query_frame.reshape(C, 2, R).transpose(1, 0, 2).reshape(1, NQ)]
where the time goes in v2:
time: 37.2 us; the launch traced here: 37 us
  Pallas kernels  36.4 us (98%)
  between operations  0.64 us (2%)
    pallas_call x1, Pallas kernels, shards(): pl.pallas_call(functools.partial(kernel, V, H), out_shape=tuple((vmem(sha...  35.5 us
    pallas_call x1, Pallas kernels, shards(): pl.pallas_call(write, out_shape=tuple((jax.ShapeDtypeStruct(shape, BF16)...  0.86 us

profile of v2, /device:TPU:0, one launch (start us, length us, event | category | flops | bytes accessed | tf_op | source)
XLA Modules:
  0.0 37.0 jit_solution(9102143508154697372)
XLA Ops:
  0.6 35.5 %shard_map.102 = (bf16[16,2048]{1,0:T(8,128)(2,1)S(1)}, bf16[512,256]{1,0:T(8,128)(2,1)S(1)}, bf16[512,256]{1,0:T(8,128)(2,1)S(1)}, bf16[32,1024]{1,0:T(8,128)(2,1)S(1)}) custom-call(s32[1,128]{1,0:T(1,128)} %bitcast.1, s32[32]{0:T(128)} %bf_ref.1, bf16[16,2048]{1,0:T(8,128)(2,1)} %q_ref.1, bf16[16,2048]{1,0:T(8,128)(2,1)} %do_ref.1, ...), custom_call_target="tpu_custom_call" | custom-call | tf_op jit(solution)/shard_map/pallas_call | solution.py:321
  36.1 0.9 %shard_map.103 = (bf16[16,2048]{1,0:T(8,128)(2,1)}, bf16[512,256]{1,0:T(8,128)(2,1)}, bf16[512,256]{1,0:T(8,128)(2,1)}, bf16[32,1024]{1,0:T(8,128)(2,1)}) custom-call(bf16[16,2048]{1,0:T(8,128)(2,1)S(1)} %get-tuple-element.8.refs_0_, bf16[512,256]{1,0:T(8,128)(2,1)S(1)} %get-tuple-element.9.refs_1_, bf16[512,256]{1,0:T(8,128)(2,1)S(1)} %get-tuple-element.10.refs_2_, ...), custom_call_target="tpu_custom_call" | custom-call | tf_op jit(solution)/shard_map/pallas_call | solution.py:361
